TPU v7x, 32 devices: a whole 2x2x4 slice. The times are simulated.
32 devices in a mesh: row: 8 (over z, x), col: 4 (over y, core).
Axes of the slice: x: 2, y: 2, z: 4, core: 2. Of those that a mesh axis runs over, the one named last changes fastest.
Arguments:
- pole_values: float32 [65536], P('row'), may hold values from -32768 to 32768, as said below
- weights: float32 [65536], P('row'), may hold values from 0.15 to 0.5
- centers: float32 [65536], P('col'), as said below
- offsets: float32 [65536], P('col'), may hold values from -0.1 to 0.1
- chosen: int32 [2048], replicated, may hold values from 0 to 65535
- column_pole: int32 [2, 32768], P(None, 'row'), may hold values from 0 to 65535, as said below
- eigen_blocks: bfloat16 [3072, 2, 32768], P('col', None, 'row'), may hold values from -6 to 6
Outputs:
- roots_offset: float32 [65536], P('col')
- panel: float32 [3072, 2, 2048], P(('col', 'row'))
Inputs may be any that keep to these rules, and one draw needn't show every extreme that they name: `pole_values`: ascending; consecutive poles differ by 1/4 to 7/4; every pole is a multiple of 1/128. centers[i] is the midpoint of pole_values[i] and pole_values[i + 1]; the last one is the last pole plus 1/2. `chosen`: indices of roots. `column_pole`: each of 0 to 65535 stands once.
All inputs are finite; a program needn't handle non-finite values.
Results may differ from a plain program's by a relative error of at most 0.0021.
Values may be sent and summed in bfloat16 or wider, within the bound.
A program may use at most 128 MiB of HBM per device.

v0:
```python
import jax
import jax.numpy as jnp
from jax import lax
from jax.sharding import PartitionSpec as P

ITERS = 3


def block_sums(pole_vals, weight_sq, center_vals, offset_vals, block_rows):
    root_count = center_vals.shape[0]
    block_rows = min(block_rows, root_count)
    center_blocks = center_vals.reshape(root_count // block_rows, block_rows)
    offset_blocks = offset_vals.reshape(root_count // block_rows, block_rows)

    def per_block(blocks):
        distance = pole_vals[None, :] - blocks[0][:, None] - blocks[1][:, None]
        inverse = 1.0 / distance
        weighted = weight_sq[None, :] * inverse
        return (
            jnp.sum(weighted, axis=1),
            jnp.sum(weighted * inverse, axis=1),
            jnp.min(jnp.abs(distance), axis=1),
        )

    sums = lax.map(per_block, (center_blocks, offset_blocks))
    return tuple((item.reshape(root_count) for item in sums))


def newton_update(offset_now, sum_inverse, sum_square, nearest):
    limit = 0.5 * nearest
    return offset_now - jnp.clip((1.0 + sum_inverse) / sum_square, -limit, limit)


def cauchy_block(pole_picked, weight_picked, panel_center, panel_offset, inv_norm):
    distance = pole_picked[:, None] - panel_center[None, :] - panel_offset[None, :]
    return (weight_picked[:, None] * (1.0 / distance) * inv_norm[None, :]).astype(jnp.bfloat16)


def on_device(pole_values, weights, centers, offsets, chosen, column_pole, eigen_blocks):
    all_poles, all_weights = (
        lax.all_gather(pole_values, "row", axis=0, tiled=True),
        lax.all_gather(weights, "row", axis=0, tiled=True),
    )
    weight_sq = weights * weights
    per_device = offsets.shape[0] // lax.axis_size("row")
    first_root = lax.axis_index("row") * per_device
    my_centers = lax.dynamic_slice_in_dim(centers, first_root, per_device)
    my_offsets = lax.dynamic_slice_in_dim(offsets, first_root, per_device)
    all_sq = all_weights * all_weights
    for iteration in range(ITERS):
        sum_inverse, sum_square, nearest = block_sums(all_poles, all_sq, my_centers, my_offsets, 32)
        my_offsets = newton_update(my_offsets, sum_inverse, sum_square, nearest)
    offset_now = lax.all_gather(my_offsets, "row", axis=0, tiled=True)
    full_centers, full_offsets = (
        lax.all_gather(centers, "col", axis=0, tiled=True),
        lax.all_gather(offset_now, "col", axis=0, tiled=True),
    )
    panel_center = full_centers[chosen]
    panel_offset = full_offsets[chosen]
    partial_sq = block_sums(pole_values, weight_sq, panel_center, panel_offset, 64)[1]
    norm_sq = lax.psum(partial_sq, "row")
    inv_norm = lax.rsqrt(norm_sq)
    cauchy_halves = []
    for half_index in range(2):
        pole_index = column_pole[half_index]
        cauchy_halves.append(
            cauchy_block(
                all_poles[pole_index], all_weights[pole_index], panel_center, panel_offset, inv_norm
            )
        )
    panel = lax.psum_scatter(
        jnp.stack(
            [
                jnp.dot(
                    eigen_blocks[:, half_index, :],
                    cauchy_halves[half_index],
                    preferred_element_type=jnp.float32,
                )
                for half_index in range(2)
            ],
            axis=1,
        ),
        "row",
        scatter_dimension=0,
        tiled=True,
    )
    return (offset_now, panel)


def solution(mesh):
    placed = (P("row"), P("row"), P("col"), P("col"), P(), P(None, "row"), P("col", None, "row"))
    return jax.shard_map(
        on_device,
        mesh=mesh,
        in_specs=placed,
        out_specs=(P("col"), P(("col", "row"), None, None)),
        check_vma=False,
    )
```

profile of v0, /device:TPU:0, one launch (start us, length us, event | category | flops | bytes accessed | tf_op | source)
XLA Modules:
  0.0 1347.6 jit_solution(16612462092690085568)
XLA Ops:
  8.1 32.8 %all_gather.15 = f32[65536]{0:T(1024)S(1)} all-gather(f32[8192]{0:T(1024)} %param.16), channel_id=1, replica_groups=mesh['row'=8,'col'=4] {'row'}, dimensions={0}, use_global_device_ids=true | all-gather | bytes 294912 | tf_op jit(solution)/shard_map/all_gather | solution.py:42
  41.7 31.0 %all_gather.16 = f32[65536]{0:T(1024)S(1)} all-gather(f32[8192]{0:T(1024)} %param.15), channel_id=1, replica_groups=mesh['row'=8,'col'=4] {'row'}, dimensions={0}, use_global_device_ids=true | all-gather | bytes 294912 | tf_op jit(solution)/shard_map/all_gather | solution.py:41
  72.7 23.0 %gather_fusion.5 = f32[4096]{0:T(1024)S(1)} fusion(f32[65536]{0:T(1024)S(1)} %all_gather.16, s32[4096]{0:T(1024)S(1)} %broadcast_clamp_fusion), kind=kCustom, calls=%fused_computation.5 | custom fusion | bytes 49152 | tf_op jit(solution)/shard_map/gather | solution.py:68
  95.7 23.0 %gather_fusion.1 = f32[4096]{0:T(1024)S(1)} fusion(f32[65536]{0:T(1024)S(1)} %all_gather.16, s32[4096]{0:T(1024)S(1)} %broadcast_clamp_fusion.1), kind=kCustom, calls=%fused_computation.1 | custom fusion | bytes 49152 | tf_op jit(solution)/shard_map/gather | solution.py:68
  118.8 23.0 %gather_fusion.4 = f32[4096]{0:T(1024)S(1)} fusion(f32[65536]{0:T(1024)S(1)} %all_gather.15, s32[4096]{0:T(1024)S(1)} %broadcast_clamp_fusion), kind=kCustom, calls=%fused_computation.4 | custom fusion | bytes 49152 | tf_op jit(solution)/shard_map/gather | solution.py:68
  141.8 23.0 %gather_fusion = f32[4096]{0:T(1024)S(1)} fusion(f32[65536]{0:T(1024)S(1)} %all_gather.15, s32[4096]{0:T(1024)S(1)} %broadcast_clamp_fusion.1), kind=kCustom, calls=%fused_computation | custom fusion | bytes 49152 | tf_op jit(solution)/shard_map/gather | solution.py:68
  164.9 5.8 all_gather.18
  171.6 184.5 %while.52 = (s32[]{:T(128)}, f32[64,32]{1,0:T(8,128)S(1)}, f32[64,32]{1,0:T(8,128)S(1)}, f32[64,32]{1,0:T(8,128)S(1)}, f32[65536]{0:T(1024)S(1)}, /*index=5*/f32...) while((s32[]{:T(128)}, f32[64,32]{1,0:T(8,128)S(1)}, ...), condition=%wide.region_4.5_spmd, body=%wide.region_0.4_spmd.sunk | while | flops 18874272 | bytes 526333 | solution.py:25
  171.6 2.7 fusion.31
  174.5 2.7 fusion.31
  177.4 2.7 fusion.31
  180.3 2.7 fusion.31
  183.1 2.7 fusion.31
  186.0 2.7 fusion.31
  188.9 2.7 fusion.31
  191.8 2.7 fusion.31
  194.7 2.7 fusion.31
  197.6 2.7 fusion.31
  200.4 2.7 fusion.31
  203.3 2.7 fusion.31
  206.2 2.7 fusion.31
  209.1 2.7 fusion.31
  212.0 2.7 fusion.31
  214.9 2.7 fusion.31
  217.7 2.7 fusion.31
  220.6 2.7 fusion.31
  263.8 2.7 fusion.31
  318.6 2.7 fusion.31
  357.0 184.5 %while.53 = (s32[]{:T(128)}, f32[64,32]{1,0:T(8,128)S(1)}, f32[64,32]{1,0:T(8,128)S(1)}, f32[64,32]{1,0:T(8,128)S(1)}, f32[65536]{0:T(1024)S(1)}, /*index=5*/f32...) while((s32[]{:T(128)}, f32[64,32]{1,0:T(8,128)S(1)}, ...), condition=%wide.region_9.10_spmd, body=%wide.region_5.9_spmd.sunk | while | flops 18874272 | bytes 526333 | solution.py:25
  406.0 2.7 fusion.32
  460.8 2.7 fusion.32
  515.6 2.7 fusion.32
  541.8 184.5 %while.54 = (s32[]{:T(128)}, f32[64,32]{1,0:T(8,128)S(1)}, f32[64,32]{1,0:T(8,128)S(1)}, f32[64,32]{1,0:T(8,128)S(1)}, f32[65536]{0:T(1024)S(1)}, /*index=5*/f32...) while((s32[]{:T(128)}, f32[64,32]{1,0:T(8,128)S(1)}, ...), condition=%wide.region_14.15_spmd, body=%wide.region_10.14_spmd.sunk | while | flops 18874272 | bytes 526333 | solution.py:25
  582.1 2.7 fusion.33
  636.9 2.7 fusion.33
  691.7 2.7 fusion.33
  726.4 30.5 %all_gather.17 = f32[16384]{0:T(1024)S(1)} all-gather(f32[2048]{0:T(1024)S(1)} %minimum_subtract_fusion), channel_id=1, replica_groups=mesh['row'=8,'col'=4] {'row'}, dimensions={0}, use_global_device_ids=true | all-gather | bytes 73728 | tf_op jit(solution)/shard_map/all_gather | solution.py:53
  756.9 5.8 all_gather.19
  762.7 11.8 gather_fusion.3
  774.6 11.8 gather_fusion.2
  786.4 21.2 %while.55 = (s32[]{:T(128)}, f32[32,64]{1,0:T(8,128)S(1)}, f32[8192]{0:T(1024)S(1)}, f32[8192]{0:T(1024)S(1)}, f32[32,64]{1,0:T(8,128)S(1)}, /*index=5*/f32[32,64]{1,0:T(8,128)S(1)}, s32[]{:T(128)}, s32[]{:T(128)}) while((s32[]{:T(128)}, f32[32,64]{1,0:T(8,128)S(1)}, f32[8192]{0:T(1024)S(1)}, f32[8192]{0:T(1024)S(1)}, ...), condition=%wide.region_17.18_spmd, body=%wide.region_15.17_spmd.sunk | while | flops 3145666 | bytes 67941 | solution.py:25
  807.7 21.6 %psum.7 = f32[2048]{0:T(1024)S(1)} all-reduce(f32[2048]{0:T(1024)S(1)} %reshape.144), channel_id=1, replica_groups=mesh['row'=8,'col'=4] {'row'}, use_global_device_ids=true, to_apply=%region_18.19 | all-reduce | flops 2048 | bytes 16384 | tf_op jit(solution)/shard_map/psum | solution.py:61
  829.3 30.3 %fusion.26 = (bf16[768,1,4096]{2,1,0:T(2,128)(2,1)}, bf16[768,1,4096]{2,1,0:T(2,128)(2,1)}) fusion(bf16[768,2,4096]{2,1,0:T(2,128)(2,1)} %param.21), kind=kLoop, calls=%fused_computation.73 | loop fusion | bytes 25165824 | tf_op jit(solution)/shard_map/slice | solution.py:75
  859.6 28.0 %fusion.22 = f32[768,1,2048]{0,2,1:T(8,128)} fusion(bf16[768,1,4096]{2,1,0:T(2,128)(2,1)} %get-tuple-element.257, f32[2048]{0:T(1024)S(1)} %rsqrt.3, f32[2048]{0:T(1024)S(1)} %gather_fusion.3, f32[2048]{0:T(1024)S(1)} %gather_fusion.2, f32[4096]{0:T(1024)S(1)} %gather_fusion.1, f32[4096]{0:T(1024)S(1)} %gather_fusion), kind=kOutput, calls=%fused_computation.54 | convolution fusion | flops 12935233536 | bytes 12640256 | tf_op jit(solution)/shard_map/dot_general | solution.py:74
  887.5 28.1 %fusion.21 = f32[768,1,2048]{0,2,1:T(8,128)} fusion(bf16[768,1,4096]{2,1,0:T(2,128)(2,1)} %get-tuple-element.258, f32[4096]{0:T(1024)S(1)} %gather_fusion.5, f32[4096]{0:T(1024)S(1)} %gather_fusion.4, f32[2048]{0:T(1024)S(1)} %rsqrt.3, f32[2048]{0:T(1024)S(1)} %gather_fusion.3, f32[2048]{0:T(1024)S(1)} %gather_fusion.2), kind=kOutput, calls=%fused_computation.53 | convolution fusion | flops 12935233536 | bytes 12640256 | tf_op jit(solution)/shard_map/dot_general | solution.py:74
  915.7 10.0 pad_maximum_fusion
  925.7 19.4 %copy.18 = f32[768,2,2048]{2,1,0:T(2,128)} copy(f32[768,2,2048]{0,2,1:T(8,128)} %pad_maximum_fusion) | data formatting | bytes 25165824 | tf_op jit(solution)/shard_map/stack | solution.py:72
  947.0 390.1 %all-reduce.3.cloned.1.call-done = f32[768,2,2048]{2,1,0:T(2,128)} async-done(((f32[768,2,2048]{2,1,0:T(2,128)}), f32[768,2,2048]{2,1,0:T(2,128)}) %all-reduce.3.cloned.1.call-update) | async-done | bytes 12582928
  (1083 shorter events, 506.9 us)
Async XLA Ops:
  7.2 1329.9 %all-reduce.3.cloned.1.call-start = ((), (), s32[]{:S(2)}) async-start(), calls=%async_computation | async-start | bytes 25165824
  141.8 23.1 %copy-start.2 = (s32[2048]{0:T(1024)S(1)}, s32[2048]{0:T(1024)}, u32[]{:S(2)}) copy-start(s32[2048]{0:T(1024)} %param.19) | copy-start | bytes 24580
  141.8 23.1 %copy-start.1 = (f32[16384]{0:T(1024)S(1)}, f32[16384]{0:T(1024)}, u32[]{:S(2)}) copy-start(f32[16384]{0:T(1024)} %param.17) | copy-start | bytes 196612
  762.7 23.7 %copy-start = (f32[8192]{0:T(1024)S(1)}, f32[8192]{0:T(1024)}, u32[]{:S(2)}) copy-start(f32[8192]{0:T(1024)} %param.15) | copy-start | bytes 98308
  945.1 0.7 copy-start.3
Sparse Core Ops, SparseCore 0:
  945.2 391.7 all-reduce.2
where the time goes:
time: 1360 us; the launch traced here: 1350 us
  other arithmetic  557 us (41%)
  waiting for transfers between devices  390 us (29%)
  local copies, waits for them, and re-layouts  196 us (14%)
  blocking collectives  127 us (9%)
  matrix products  56.1 us (4%)
  between operations  15.4 us (1%)
    reduce_sum x224, other arithmetic, per_block(): jnp.sum(weighted * inverse, axis=1)  545 us
    unnamed x2, waiting for transfers between devices  390 us
    dot_general x2, matrix products, on_device(): jnp.dot(eigen_blocks[:, half_index, :], cauchy_halves[half_index], prefer...  56.1 us
    gather x2, local copies, waits for them, and re-layouts, on_device(): all_weights[pole_index]  46.1 us
    gather x2, local copies, waits for them, and re-layouts, on_device(): all_poles[pole_index]  46.1 us
    all_gather x1, blocking collectives, on_device(): lax.all_gather(weights, 'row', axis=0, tiled=True)  32.8 us
    all_gather x1, blocking collectives, on_device(): lax.all_gather(pole_values, 'row', axis=0, tiled=True)  31 us
    all_gather x1, blocking collectives, on_device(): offset_now = lax.all_gather(my_offsets, 'row', axis=0, tiled=True)  30.5 us
  transfers between devices with their start and end apart: 1, of which 1 were waited for; matrix products, arithmetic and copies ran while one was open for 0% of the time, Pallas kernels for 0%

commit v1 on v0

v1 whole, which is shorter than its diff:
```python
import jax
import jax.numpy as jnp
from jax import lax
from jax.experimental import pallas as pl
from jax.experimental.pallas import tpu as pltpu
from jax.sharding import PartitionSpec as P

ITERS = 3
LANES = 128
GROUP = 4


def pole_sweep(bases_ref, poles_ref, weight_sq_ref, center, offset, square_only):
    tiles = center.shape[0]

    def block(index, sums):
        base = bases_ref[index]
        relative = poles_ref[pl.ds(index, 1), :] - base
        pole_t = jnp.broadcast_to(relative, (LANES, LANES)).T
        weight_t = jnp.broadcast_to(weight_sq_ref[pl.ds(index, 1), :], (LANES, LANES)).T
        root = (center - base) + offset
        inverse_sums, square_sums = list(sums[0]), list(sums[1])
        for first in range(0, tiles, GROUP):
            members = range(first, min(first + GROUP, tiles))
            points = {m: jnp.broadcast_to(root[m : m + 1, :], (8, LANES)) for m in members}
            part_inverse = {m: None for m in members}
            part_square = {m: None for m in members}
            for k in range(LANES // 8):
                pole = pole_t[8 * k : 8 * k + 8, :]
                weight = weight_t[8 * k : 8 * k + 8, :]
                for m in members:
                    inverse = 1.0 / (pole - points[m])
                    weighted = weight * inverse
                    square = weighted * inverse
                    if k == 0:
                        part_inverse[m], part_square[m] = weighted, square
                    else:
                        part_inverse[m] = part_inverse[m] + weighted
                        part_square[m] = part_square[m] + square
            for m in members:
                inverse_sums[m] = inverse_sums[m] + part_inverse[m]
                square_sums[m] = square_sums[m] + part_square[m]
        if square_only:
            inverse_sums = list(sums[0])
        return tuple(inverse_sums), tuple(square_sums)

    zero = tuple(jnp.zeros((8, LANES), jnp.float32) for _ in range(tiles))
    inverse_sums, square_sums = lax.fori_loop(0, poles_ref.shape[0], block, (zero, zero))
    fold = lambda parts: jnp.concatenate([jnp.sum(p, axis=0, keepdims=True) for p in parts], axis=0)
    return None if square_only else fold(inverse_sums), fold(square_sums)


def roots_kernel(bases_ref, poles_ref, weight_sq_ref, center_ref, offset_ref, left_ref, right_ref, out_ref):
    center = center_ref[...]
    to_left = left_ref[...] - center
    to_right = right_ref[...] - center

    def step(_, offset):
        sum_inverse, sum_square = pole_sweep(bases_ref, poles_ref, weight_sq_ref, center, offset, False)
        limit = 0.5 * jnp.minimum(jnp.abs(to_left - offset), jnp.abs(to_right - offset))
        change = (1.0 + sum_inverse) / sum_square
        return offset - jnp.minimum(jnp.maximum(change, -limit), limit)

    out_ref[...] = lax.fori_loop(0, ITERS, step, offset_ref[...])


def norm_kernel(bases_ref, poles_ref, weight_sq_ref, center_ref, offset_ref, out_ref):
    out_ref[...] = pole_sweep(
        bases_ref, poles_ref, weight_sq_ref, center_ref[...], offset_ref[...], True
    )[1]


def run_kernel(kernel, bases, *operands):
    vmem = pl.BlockSpec(memory_space=pltpu.VMEM)
    return pl.pallas_call(
        kernel,
        out_shape=jax.ShapeDtypeStruct(operands[2].shape, jnp.float32),
        in_specs=[pl.BlockSpec(memory_space=pltpu.SMEM)] + [vmem] * len(operands),
        out_specs=vmem,
    )(bases, *operands)


def lookup(tables, index):
    rows = jnp.concatenate([t.reshape(-1, LANES) for t in tables], axis=1)
    high = lax.reduce_precision(rows, 8, 7)
    middle = lax.reduce_precision(rows - high, 8, 7)
    low = (rows - high) - middle
    pieces = jnp.concatenate([high, middle, low], axis=1).astype(jnp.bfloat16)
    pick = (index[:, None] // LANES == jnp.arange(rows.shape[0])[None, :]).astype(jnp.bfloat16)
    found = jnp.dot(pick, pieces, preferred_element_type=jnp.float32)
    width = rows.shape[1]
    found = (found[:, :width] + found[:, width : 2 * width]) + found[:, 2 * width :]
    lane = index[:, None] % LANES == jnp.arange(LANES)[None, :]
    return [
        jnp.sum(jnp.where(lane, found[:, t * LANES : (t + 1) * LANES], 0.0), axis=1)
        for t in range(len(tables))
    ]


def on_device(pole_values, weights, centers, offsets, chosen, column_pole, eigen_blocks):
    gathered = lax.all_gather(jnp.stack([pole_values, weights]), "row", axis=1, tiled=True)
    all_poles, all_weights = gathered[0], gathered[1]
    rows = lax.axis_size("row")
    per_device = offsets.shape[0] // rows
    first_root = lax.axis_index("row") * per_device
    my_first = lax.axis_index("col") * offsets.shape[0] + first_root
    my_centers = lax.dynamic_slice_in_dim(centers, first_root, per_device)
    my_offsets = lax.dynamic_slice_in_dim(offsets, first_root, per_device)
    shifted = jnp.concatenate([all_poles[1:], all_poles[-1:]])
    left = lax.dynamic_slice_in_dim(all_poles, my_first, per_device)
    right = lax.dynamic_slice_in_dim(shifted, my_first, per_device)

    flat = lambda values: values.reshape(-1, LANES)
    pole_rows = flat(all_poles)
    my_offsets = run_kernel(
        roots_kernel,
        pole_rows[:, LANES // 2],
        pole_rows,
        flat(all_weights * all_weights),
        flat(my_centers),
        flat(my_offsets),
        flat(left),
        flat(right),
    ).reshape(-1)

    match = (chosen[:, None] - my_first) == jnp.arange(per_device)[None, :]
    picked = jnp.stack(
        [
            jnp.sum(jnp.where(match, my_centers[None, :], 0.0), axis=1),
            jnp.sum(jnp.where(match, my_offsets[None, :], 0.0), axis=1),
        ]
    )
    panel_center, panel_offset = lax.psum(picked, ("row", "col"))
    offset_now = lax.all_gather(my_offsets, "row", axis=0, tiled=True)
    local_rows = flat(pole_values)
    partial_sq = run_kernel(
        norm_kernel,
        local_rows[:, LANES // 2],
        local_rows,
        flat(weights * weights),
        flat(panel_center),
        flat(panel_offset),
    ).reshape(-1)
    inv_norm = lax.rsqrt(lax.psum(partial_sq, "row"))

    pole_picked, weight_picked = lookup([all_poles, all_weights], column_pole.reshape(-1))
    pole_picked = pole_picked.reshape(column_pole.shape)
    weight_picked = weight_picked.reshape(column_pole.shape)
    halves = []
    for half in range(column_pole.shape[0]):
        distance = (pole_picked[half][:, None] - panel_center[None, :]) - panel_offset[None, :]
        cauchy = (weight_picked[half][:, None] * (1.0 / distance) * inv_norm[None, :]).astype(jnp.bfloat16)
        part = jnp.dot(eigen_blocks[:, half, :], cauchy, preferred_element_type=jnp.float32)
        sent = part.astype(jnp.bfloat16).reshape(rows, -1, part.shape[1])
        got = lax.all_to_all(sent, "row", split_axis=0, concat_axis=0, tiled=True)
        halves.append(jnp.sum(got.astype(jnp.float32), axis=0))
    return (offset_now, jnp.stack(halves, axis=1))


def solution(mesh):
    placed = (P("row"), P("row"), P("col"), P("col"), P(), P(None, "row"), P("col", None, "row"))
    return jax.shard_map(
        on_device,
        mesh=mesh,
        in_specs=placed,
        out_specs=(P("col"), P(("col", "row"), None, None)),
        check_vma=False,
    )
```

time: 1360 us -> 847 us (0.62)
  other arithmetic: 557 us -> 27.2 us
  Pallas kernels: 0 us -> 472 us
  waiting for transfers between devices: 390 us -> 41.4 us
  local copies, waits for them, and re-layouts: 196 us -> 41.4 us
  blocking collectives: 127 us -> 184 us
  between operations: 15.4 us -> 1.28 us
    reduce_sum x224 -> x4, other arithmetic: 545 us -> 11.2 us  [the longest x1 6.34 us: on_device(): jnp.sum(jnp.where(match, my_centers[None, :], 0.0), axis=1)]
    pallas_call x0 -> x2, Pallas kernels: none -> 472 us  [run_kernel(): pl.pallas_call(kernel, out_shape=jax.ShapeDtypeStruct(operands[2].shape,...]
    unnamed x2 -> x0, waiting for transfers between devices: 390 us -> none
    gather x6 -> x0, local copies, waits for them, and re-layouts: 116 us -> none  [the longest x2 46.1 us: on_device(): all_weights[pole_index]]
    all_gather x1, blocking collectives: 30.5 us -> 89.9 us  [on_device(): offset_now = lax.all_gather(my_offsets, 'row', axis=0, tiled=True)]
    all_gather x4 -> x1, blocking collectives: 75.3 us -> 33 us  [on_device(): lax.all_gather(jnp.stack([pole_values, weights]), 'row', axis=1, tiled=True)]
    all_to_all x0 -> x2, waiting for transfers between devices: none -> 41.4 us  [on_device(): got = lax.all_to_all(sent, 'row', split_axis=0, concat_axis=0, tiled=True)]
    psum x1 -> x2, blocking collectives: 21.6 us -> 60.5 us  [the longest x1 39.8 us: on_device(): panel_center, panel_offset = lax.psum(picked, ('row', 'col'))]
  transfers between devices with their start and end apart: 1 -> 2, of which waited for: 1 -> 1; matrix products, arithmetic and copies ran while one was open for 0% -> 3% of each run, Pallas kernels for 0% -> 0%
where the time goes in v1:
time: 847 us; the launch traced here: 834 us
  Pallas kernels  472 us (56%)
  blocking collectives  184 us (22%)
  matrix products  59.7 us (7%)
  local copies, waits for them, and re-layouts  41.4 us (5%)
  waiting for transfers between devices  41.4 us (5%)
  other arithmetic  27.2 us (3%)
    pallas_call x2, Pallas kernels, run_kernel(): pl.pallas_call(kernel, out_shape=jax.ShapeDtypeStruct(operands[2].shape,...  472 us
    all_gather x1, blocking collectives, on_device(): offset_now = lax.all_gather(my_offsets, 'row', axis=0, tiled=True)  89.9 us
    dot_general x2, matrix products, on_device(): jnp.dot(eigen_blocks[:, half, :], cauchy, preferred_element_type=jnp.floa...  48.4 us
    all_to_all x2, waiting for transfers between devices, on_device(): got = lax.all_to_all(sent, 'row', split_axis=0, concat_axis=0, tiled=True)  41.4 us
    psum x1, blocking collectives, on_device(): panel_center, panel_offset = lax.psum(picked, ('row', 'col'))  39.8 us
    all_gather x1, blocking collectives, on_device(): lax.all_gather(jnp.stack([pole_values, weights]), 'row', axis=1, tiled=True)  33 us
    slice x1, local copies, waits for them, and re-layouts, on_device(): eigen_blocks[:, half, :]  29.5 us
    psum x1, blocking collectives, on_device(): inv_norm = lax.rsqrt(lax.psum(partial_sq, 'row'))  20.7 us
  transfers between devices with their start and end apart: 2, of which 1 were waited for; matrix products, arithmetic and copies ran while one was open for 3% of the time, Pallas kernels for 0%

profile of v1, /device:TPU:0, one launch (start us, length us, event | category | flops | bytes accessed | tf_op | source)
XLA Modules:
  0.0 834.3 jit_solution(719434560128669392)
XLA Ops:
  0.6 0.8 pad_maximum_fusion.2
  1.5 33.0 %all_gather.6 = f32[2,65536]{1,0:T(2,128)S(1)} all-gather(f32[2,8192]{1,0:T(2,128)S(1)} %pad_maximum_fusion.2), channel_id=1, replica_groups=mesh['row'=8,'col'=4] {'row'}, dimensions={1}, use_global_device_ids=true | all-gather | bytes 589824 | tf_op jit(solution)/shard_map/all_gather | solution.py:101
  34.5 0.6 slice.85
  35.1 0.6 slice.86
  35.7 0.4 fusion.34
  36.1 0.0 copy-start
  36.1 1.3 dynamic-slice_bitcast_fusion.1.center_ref
  37.5 0.7 dynamic_slice.12
  38.2 1.4 multiply_bitcast_fusion.weight_sq_ref
  39.5 0.8 slice_reduce_fusion.bases_ref
  40.4 0.7 mul.43.weight_sq_ref
  41.1 0.1 reduce-precision_convert_fusion.1
  41.2 0.6 constant_dynamic-slice_fusion
  41.8 0.7 broadcast_subtract_fusion
  42.5 1.9 dynamic-slice_bitcast_fusion
  44.5 453.9 %shard_map.86 = f32[16,128]{1,0:T(8,128)} custom-call(f32[512]{0:T(512)} %slice_reduce_fusion.bases_ref, f32[512,128]{1,0:T(8,128)} %bitcast.48, f32[512,128]{1,0:T(8,128)} %mul.43.weight_sq_ref, f32[16,128]{1,0:T(8,128)} %dynamic-slice_bitcast_fusion.1.center_ref, f32[16,128]{1,0:T(8,128)} %get-tuple-element.27.offset_ref, f32[16,128]{1,0:T(8,128)} %bitcast.64, ...), custom_call_target="tpu_custom_call" | custom-call | tf_op jit(solution)/shard_map/pallas_call | solution.py:75
  498.4 6.3 select_reduce_fusion.1
  504.7 39.8 %psum.14 = f32[2,2048]{1,0:T(2,128)S(1)} all-reduce(f32[2,2048]{1,0:T(2,128)S(1)} %pad_maximum_fusion.3), channel_id=1, replica_groups=mesh['row'=8,'col'=4] {'row','col'}, use_global_device_ids=true, to_apply=%region_4.5 | all-reduce | flops 4096 | bytes 32768 | tf_op jit(solution)/shard_map/psum | solution.py:133
  544.5 0.6 fusion.37
  545.1 1.4 slice_reduce_fusion.1.bases_ref
  546.6 17.7 %shard_map.87 = f32[16,128]{1,0:T(8,128)} custom-call(f32[64]{0:T(128)} %slice_reduce_fusion.1.bases_ref, f32[64,128]{1,0:T(8,128)} %bitcast.59, f32[64,128]{1,0:T(8,128)} %multiply_bitcast_fusion.weight_sq_ref, f32[16,128]{1,0:T(8,128)} %bitcast.70, f32[16,128]{1,0:T(8,128)} %bitcast.67), custom_call_target="tpu_custom_call" | custom-call | tf_op jit(solution)/shard_map/pallas_call | solution.py:75
  564.3 20.7 %psum.15 = f32[2048]{0:T(1024)S(1)} all-reduce(f32[2048]{0:T(1024)} %bitcast.66), channel_id=1, replica_groups=mesh['row'=8,'col'=4] {'row'}, use_global_device_ids=true, to_apply=%region_5.6 | all-reduce | flops 2048 | bytes 16384 | tf_op jit(solution)/shard_map/psum | solution.py:144
  585.1 0.6 rsqrt.3
  585.7 0.8 copy.20
  586.5 0.0 slice-start
  586.5 0.0 slice-start.1
  586.5 11.4 %fusion.14 = f32[8192,768]{0,1:T(8,128)} fusion(s32[8192]{0:T(1024)S(1)} %get-tuple-element.24, bf16[512,256]{1,0:T(8,128)(2,1)S(1)} %get-tuple-element.16, bf16[512,256]{1,0:T(8,128)(2,1)S(1)} %get-tuple-element.15, bf16[512,256]{1,0:T(8,128)(2,1)S(1)} %get-tuple-element.14), kind=kOutput, calls=%fused_computation.20 | convolution fusion | flops 6449004544 | bytes 25985024 | tf_op jit(solution)/shard_map/dot_general | solution.py:90
  597.9 9.0 %slice_add_fusion = f32[8192,256]{0,1:T(8,128)S(1)} fusion(f32[8192,768]{0,1:T(8,128)} %fusion.14), kind=kLoop, calls=%fused_computation.21 | loop fusion | flops 4194304 | bytes 33554432 | tf_op jit(solution)/shard_map/add | solution.py:92
  606.9 0.0 slice-done
  606.9 0.0 slice-done.1
  606.9 0.4 slice-done.2
  607.3 29.5 %fusion.33 = (bf16[768,1,4096]{2,1,0:T(2,128)(2,1)}, bf16[768,1,4096]{2,1,0:T(2,128)(2,1)}) fusion(bf16[768,2,4096]{2,1,0:T(2,128)(2,1)S(1)} %bitcast.45), kind=kLoop, calls=%fused_computation.69 | loop fusion | bytes 25165824 | tf_op jit(solution)/shard_map/slice | solution.py:153
  636.8 0.9 fusion.17
  637.7 0.0 copy-done.2
  637.7 0.0 copy-start.3
  637.7 0.0 copy-start.4
  637.7 24.2 %fusion.19 = bf16[2048,768]{0,1:T(8,128)(2,1)} fusion(f32[2048]{0:T(1024)} %rsqrt.3, f32[2048]{0:T(1024)S(1)} %bitcast.68, f32[2048]{0:T(1024)} %bitcast.71, f32[4096]{0:T(1024)S(1)} %get-tuple-element.30, f32[4096]{0:T(1024)S(1)} %get-tuple-element.19, bf16[768,1,4096]{2,1,0:T(2,128)(2,1)} %get-tuple-element.12), kind=kOutput, calls=%fused_computation.34 | convolution fusion | flops 12936806400 | bytes 9494528 | tf_op jit(solution)/shard_map/dot_general | solution.py:153
  661.9 3.6 all-to-all-start
  665.6 24.2 %fusion.18 = bf16[2048,768]{0,1:T(8,128)(2,1)} fusion(f32[4096]{0:T(1024)S(1)} %get-tuple-element.29, f32[4096]{0:T(1024)S(1)} %get-tuple-element.20, f32[2048]{0:T(1024)S(1)} %copy-done.4, f32[2048]{0:T(1024)S(1)} %bitcast.69, f32[2048]{0:T(1024)S(1)} %bitcast.72, bf16[768,1,4096]{2,1,0:T(2,128)(2,1)} %get-tuple-element.13), kind=kOutput, calls=%fused_computation.33 | convolution fusion | flops 12936806400 | bytes 9494528 | tf_op jit(solution)/shard_map/dot_general | solution.py:153
  689.8 41.4 %all-to-all-done = bf16[8,96,2048]{2,1,0:T(8,128)(2,1)S(1)} async-done(((bf16[8,96,2048]{2,1,0:T(8,128)(2,1)}), bf16[8,96,2048]{2,1,0:T(8,128)(2,1)S(1)}, u32[]{:S(2)}, u32[]{:S(2)}) %all-to-all-start) | async-done | bytes 3145760 | tf_op jit(solution)/shard_map/all_to_all | solution.py:155
  731.2 4.4 all-to-all-start.1
  735.6 89.9 %all_gather.7 = f32[16384]{0:T(1024)S(1)} all-gather(f32[2048]{0:T(1024)S(1)} %bitcast.63), channel_id=1, replica_groups=mesh['row'=8,'col'=4] {'row'}, dimensions={0}, use_global_device_ids=true | all-gather | bytes 73728 | tf_op jit(solution)/shard_map/all_gather | solution.py:134
  825.6 1.4 convert_reduce_fusion.1
  827.0 0.0 all-to-all-done.1
  827.0 2.5 convert_reduce_fusion
  829.6 1.2 pad_maximum_fusion
  830.8 2.4 copy.17
  833.2 0.6 copy.30
  (11 shorter events, 0.1 us)
Async XLA Ops:
  36.1 8.3 %copy-start = (f32[1,65536]{1,0:T(1,128)}, f32[1,65536]{1,0:T(1,128)S(1)}, u32[]{:S(2)}) copy-start(f32[1,65536]{1,0:T(1,128)S(1)} %get-tuple-element.18) | copy-start | bytes 786436
  586.5 20.4 %slice-start = ((s8[12582912]{0:T(1024)(128)(4,1)}), s8[4194304]{0:T(1024)(128)(4,1)S(1)}, s32[]{:S(2)}) async-start(s8[12582912]{0:T(1024)(128)(4,1)} %bitcast.44), calls=%async_computation.2 | async-start | bytes 8388608
  586.5 20.4 %slice-start.1 = ((s8[12582912]{0:T(1024)(128)(4,1)}), s8[4194304]{0:T(1024)(128)(4,1)S(1)}, s32[]{:S(2)}) async-start(s8[12582912]{0:T(1024)(128)(4,1)} %bitcast.44), calls=%async_computation.3 | async-start | bytes 8388608
  597.9 9.4 %slice-start.2 = ((s8[12582912]{0:T(1024)(128)(4,1)}), s8[4194304]{0:T(1024)(128)(4,1)S(1)}, s32[]{:S(2)}) async-start(s8[12582912]{0:T(1024)(128)(4,1)} %bitcast.44), calls=%async_computation.4 | async-start | bytes 8388608
  607.3 30.4 %copy-start.2 = (f32[1,2048]{1,0:T(1,128)S(1)}, f32[1,2048]{1,0:T(1,128)}, u32[]{:S(2)}) copy-start(f32[1,2048]{1,0:T(1,128)} %get-tuple-element.25) | copy-start | bytes 24580
  637.7 27.9 %copy-start.3 = (f32[1,2048]{1,0:T(1,128)S(1)}, f32[1,2048]{1,0:T(1,128)}, u32[]{:S(2)}) copy-start(f32[1,2048]{1,0:T(1,128)} %get-tuple-element.26) | copy-start | bytes 24580
  637.7 27.9 %copy-start.4 = (f32[2048]{0:T(1024)S(1)}, f32[2048]{0:T(1024)}, u32[]{:S(2)}) copy-start(f32[2048]{0:T(1024)} %rsqrt.3) | copy-start | bytes 24580
  661.9 69.3 %all-to-all-start = ((bf16[8,96,2048]{2,1,0:T(8,128)(2,1)}), bf16[8,96,2048]{2,1,0:T(8,128)(2,1)S(1)}, u32[]{:S(2)}, u32[]{:S(2)}) async-start(bf16[8,96,2048]{2,1,0:T(8,128)(2,1)} %bitcast.53), calls=%async_computation | async-start | bytes 6291456 | tf_op jit(solution)/shard_map/all_to_all | solution.py:155
  665.6 70.0 %copy-start.1 = (f32[16,128]{1,0:T(8,128)S(1)}, f32[16,128]{1,0:T(8,128)}, u32[]{:S(2)}) copy-start(f32[16,128]{1,0:T(8,128)} %shard_map.86) | copy-start | bytes 24580
  731.2 95.8 %all-to-all-start.1 = ((bf16[8,96,2048]{2,1,0:T(8,128)(2,1)}), bf16[8,96,2048]{2,1,0:T(8,128)(2,1)}, u32[]{:S(2)}, u32[]{:S(2)}) async-start(bf16[8,96,2048]{2,1,0:T(8,128)(2,1)} %bitcast.52), calls=%async_computation.1 | async-start | bytes 6291456 | tf_op jit(solution)/shard_map/all_to_all | solution.py:155
